TPU v7x, 32 devices: a whole 2x2x4 slice. The times are simulated.
32 devices in a mesh: member: 8 (over y, x, core), lat: 4 (over z).
Axes of the slice: x: 2, y: 2, z: 4, core: 2. Of those that a mesh axis runs over, the one named last changes fastest.
Arguments:
- ensemble: float32 [16, 3, 1, 32, 1440], P('member', None, None, 'lat'), may hold values from -6 to 6
- observation: float32 [3, 1, 32, 1440], P(None, None, 'lat'), may hold values from -6 to 6
- valid_mask: int32 [16], P('member'), may hold values from 0 to 1, as said below
- band_start: int32 [4], P('lat'), may hold values from 0 to 713
Outputs:
- crps_field: float32 [3, 1, 32, 1440], P(None, None, ('lat', 'member'))
- score_table: float32 [3, 1], replicated
Inputs may be any that keep to these rules, and one draw needn't show every extreme that they name: `valid_mask`: exactly 13 entries are 1, at positions drawn afresh.
All inputs are finite; a program needn't handle non-finite values.
Results may differ from a plain program's by a relative error of at most 0.0001.
Values sent between devices are 32-bit elements; how exact they have to be, the bound alone decides.
A program may use at most 64 MiB of HBM per device.

v0:
```python
import math
import jax
import jax.numpy as jnp
from jax import lax
from jax.sharding import PartitionSpec as P

GRID_LAT = 721
GRID_LON = 1440


def on_device(ensemble, observation, valid_mask, band_start):
    member_flags = valid_mask.astype(jnp.float32)
    lat_rows = ensemble.shape[3]
    block_rows = lat_rows // lax.axis_size("member")
    row_offset = lax.axis_index("member") * block_rows
    members = lax.all_to_all(ensemble, "member", split_axis=3, concat_axis=0, tiled=True)
    all_flags = lax.all_gather(member_flags, "member", axis=0, tiled=True)
    slot_total = members.shape[0]
    truth_slice = lax.dynamic_slice_in_dim(observation, row_offset, block_rows, 2)
    valid_count = jnp.sum(all_flags)
    flag_column = all_flags[:, None, None, None, None]
    skill_term = jnp.sum(flag_column * jnp.abs(members - truth_slice[None]), axis=0)
    group_count = slot_total // 8
    blocks = members.reshape((group_count, 8) + members.shape[1:])
    block_flags = all_flags.reshape(group_count, 8)

    def block_sum(block_item):
        block_slab, flags_here = block_item

        def add_one(position, running_sum):
            one_slab = lax.dynamic_index_in_dim(block_slab, position, 0, keepdims=True)
            one_flag = lax.dynamic_index_in_dim(flags_here, position, 0, keepdims=False)
            return running_sum + one_flag * jnp.sum(
                flag_column * jnp.abs(one_slab - members), axis=0
            )

        return lax.fori_loop(0, 8, add_one, jnp.zeros(truth_slice.shape, jnp.float32))

    spread = jnp.sum(lax.map(block_sum, (blocks, block_flags)), axis=0)
    crps_field = skill_term / valid_count - spread / (2.0 * valid_count * (valid_count - 1.0))
    row_index = (band_start[0] + row_offset + jnp.arange(block_rows, dtype=jnp.int32)).astype(
        jnp.float32
    )
    weight = jnp.cos((90.0 - row_index * 180.0 / (GRID_LAT - 1)) * math.pi / 180.0)
    partial_sums = jnp.sum(crps_field * weight[:, None], axis=(2, 3))
    totals = lax.psum(partial_sums, ("member", "lat"))
    score_table = totals / (lax.axis_size("lat") * lat_rows * GRID_LON)
    return (crps_field, score_table)


def solution(mesh):
    placed = (
        P("member", None, None, "lat", None),
        P(None, None, "lat", None),
        P("member"),
        P("lat"),
    )
    return jax.shard_map(
        on_device,
        mesh=mesh,
        in_specs=placed,
        out_specs=(P(None, None, ("lat", "member"), None), P()),
        check_vma=False,
    )
```

profile of v0, /device:TPU:0, one launch (start us, length us, event | category | flops | bytes accessed | tf_op | source)
XLA Modules:
  0.0 100.7 jit_solution(13239071511892019307)
XLA Ops:
  0.6 1.9 %copy.26 = f32[2,3,1,8,1440]{4,1,2,0,3:T(4,128)} copy(f32[2,3,1,8,1440]{4,3,2,1,0:T(8,128)} %param.8) | data formatting | bytes 552960 | tf_op args[0]
  2.6 5.2 %all-to-all-start = ((f32[2,3,1,8,1440]{4,1,2,0,3:T(4,128)}), f32[2,3,1,8,1440]{4,1,2,0,3:T(4,128)S(1)}, u32[]{:S(2)}, u32[]{:S(2)}) async-start(f32[2,3,1,8,1440]{4,1,2,0,3:T(4,128)} %copy.26), calls=%async_computation | async-start | bytes 786432 | tf_op jit(solution)/shard_map/all_to_all | solution.py:16
  7.8 0.6 copy-done.2
  8.4 0.6 dynamic-slice
  9.7 0.6 copy-done.1
  10.4 14.4 %all-reduce = f32[16]{0:T(128)S(1)} all-reduce(f32[16]{0:T(128)S(1)} %convert_dynamic-update-slice_fusion), channel_id=1, replica_groups=mesh['member'=8,'lat'=4] {'member'}, use_global_device_ids=true, to_apply=%add | all-reduce | flops 16 | bytes 128
  25.0 0.7 reduce_sum.50
  27.8 0.2 multiply_reduce_fusion.1
  28.0 0.3 copy.28
  28.3 31.1 %while.25 = (s32[]{:T(128)}, f32[2,3,1,1,1440]{4,3,2,1,0:T(1,128)S(1)}, f32[2,8,3,1,1,1440]{5,4,3,2,1,0:T(1,128)S(1)}, f32[2,8]{1,0:T(2,128)S(1)}, f32[16,1,1,1,...) while((s32[]{:T(128)}, ...), condition=%wide.region_6.7_spmd, body=%wide.region_2.6_spmd.sunk | while | flops 285125 | bytes 780332 | solution.py:39
  28.4 15.4 %while.26 = (s32[]{:T(128)}, f32[3,1,1,1440]{3,2,1,0:T(1,128)S(1)}, f32[8]{0:T(128)S(1)}, f32[16,1,1,1,1]{0,4,3,2,1:T(1,128)S(1)}, f32[8,3,1,1,1440]{4,3,2,1,0:T...) while((s32[]{:T(128)}, f32[3,1,1,1440]{3,2,1,0:T(1,128)S(1)}, ...), condition=%wide.region_5.5_spmd.clone, body=%wide.region_3.4_spmd.clone.sunk | while | flops 285123 | bytes 466739 | solution.py:37
  28.4 0.5 multiply_reduce_fusion.4
  28.9 0.7 dynamic_slice.43
  29.6 0.7 broadcast_multiply_fusion.3
  30.4 0.5 multiply_reduce_fusion.4
  30.8 0.7 dynamic_slice.43
  31.5 0.7 broadcast_multiply_fusion.3
  32.3 0.5 multiply_reduce_fusion.4
  32.8 0.7 dynamic_slice.43
  33.4 0.7 broadcast_multiply_fusion.3
  34.2 0.5 multiply_reduce_fusion.4
  34.7 0.7 dynamic_slice.43
  35.4 0.7 broadcast_multiply_fusion.3
  36.2 0.5 multiply_reduce_fusion.4
  36.6 0.7 dynamic_slice.43
  37.3 0.7 broadcast_multiply_fusion.3
  38.1 0.5 multiply_reduce_fusion.4
  38.6 0.7 dynamic_slice.43
  39.2 0.7 broadcast_multiply_fusion.3
  40.0 0.5 multiply_reduce_fusion.4
  40.5 0.7 dynamic_slice.43
  41.2 0.7 broadcast_multiply_fusion.3
  41.9 0.5 multiply_reduce_fusion.4
  42.4 0.7 dynamic_slice.43
  43.1 0.7 broadcast_multiply_fusion.3
  43.9 15.4 %while.26 = (s32[]{:T(128)}, f32[3,1,1,1440]{3,2,1,0:T(1,128)S(1)}, f32[8]{0:T(128)S(1)}, f32[16,1,1,1,1]{0,4,3,2,1:T(1,128)S(1)}, f32[8,3,1,1,1440]{4,3,2,1,0:T...) while((s32[]{:T(128)}, f32[3,1,1,1440]{3,2,1,0:T(1,128)S(1)}, ...), condition=%wide.region_5.5_spmd.clone, body=%wide.region_3.4_spmd.clone.sunk | while | flops 285123 | bytes 466739 | solution.py:37
  44.0 0.5 multiply_reduce_fusion.4
  44.4 0.7 dynamic_slice.43
  45.1 0.7 broadcast_multiply_fusion.3
  45.9 0.5 multiply_reduce_fusion.4
  46.4 0.7 dynamic_slice.43
  47.0 0.7 broadcast_multiply_fusion.3
  47.8 0.5 multiply_reduce_fusion.4
  48.3 0.7 dynamic_slice.43
  49.0 0.7 broadcast_multiply_fusion.3
  49.8 0.5 multiply_reduce_fusion.4
  50.2 0.7 dynamic_slice.43
  50.9 0.7 broadcast_multiply_fusion.3
  51.7 0.5 multiply_reduce_fusion.4
  52.2 0.7 dynamic_slice.43
  52.8 0.7 broadcast_multiply_fusion.3
  53.6 0.5 multiply_reduce_fusion.4
  54.1 0.7 dynamic_slice.43
  54.8 0.7 broadcast_multiply_fusion.3
  55.6 0.5 multiply_reduce_fusion.4
  56.0 0.7 dynamic_slice.43
  56.7 0.7 broadcast_multiply_fusion.3
  57.5 0.5 multiply_reduce_fusion.4
  57.9 0.7 dynamic_slice.43
  58.6 0.7 broadcast_multiply_fusion.3
  59.5 0.8 multiply_reduce_fusion.2
  60.2 0.6 sub.70
  60.8 39.4 %psum.7 = f32[3,1]{0,1:T(1,128)S(1)} all-reduce(f32[3,1]{0,1:T(1,128)S(1)} %bitcast.50), channel_id=1, replica_groups=mesh['member'=8,'lat'=4] {'member','lat'}, use_global_device_ids=true, to_apply=%region_9.10 | all-reduce | flops 3 | bytes 24 | tf_op jit(solution)/shard_map/psum | solution.py:46
  100.2 0.5 broadcast_multiply_fusion.1
  (70 shorter events, 1.6 us)
Async XLA Ops:
  0.6 25.0 %copy-start = (f32[3,1,8,1440]{3,2,1,0:T(8,128)S(1)}, f32[3,1,8,1440]{3,2,1,0:T(8,128)}, u32[]{:S(2)}) copy-start(f32[3,1,8,1440]{3,2,1,0:T(8,128)} %param.9) | copy-start | bytes 414724
  2.6 25.2 %all-to-all-start = ((f32[2,3,1,8,1440]{4,1,2,0,3:T(4,128)}), f32[2,3,1,8,1440]{4,1,2,0,3:T(4,128)S(1)}, u32[]{:S(2)}, u32[]{:S(2)}) async-start(f32[2,3,1,8,1440]{4,1,2,0,3:T(4,128)} %copy.26), calls=%async_computation | async-start | bytes 786432 | tf_op jit(solution)/shard_map/all_to_all | solution.py:16
  7.8 0.7 copy-start.2
  9.7 0.7 copy-start.1
where the time goes:
time: 101 us
  blocking collectives  53.8 us (53%)
  other arithmetic  21.6 us (21%)
  local copies, waits for them, and re-layouts  16.1 us (16%)
  starting transfers between devices  5.2 us (5%)
  between operations  3.34 us (3%)
    psum x1, blocking collectives, on_device(): totals = lax.psum(partial_sums, ('member', 'lat'))  39.4 us
    unnamed x1, blocking collectives  14.4 us
    mul x16, other arithmetic, add_one(): one_flag * jnp.sum(flag_column * jnp.abs(one_slab - members), axis=0)  11.1 us
    dynamic_slice x16, local copies, waits for them, and re-layouts, add_one(): one_flag = lax.dynamic_index_in_dim(flags_here, position, 0, keepdims=False)  10.7 us
    reduce_sum x16, other arithmetic, add_one(): jnp.sum(flag_column * jnp.abs(one_slab - members), axis=0)  7.4 us
    all_to_all x1, starting transfers between devices, on_device(): lax.all_to_all(ensemble, 'member', split_axis=3, concat_axis=0, tiled=True)  5.2 us
    unnamed x10, local copies, waits for them, and re-layouts  3.83 us
  transfers between devices with their start and end apart: 1, of which 0 were waited for; matrix products, arithmetic and copies ran while one was open for 2% of the time, Pallas kernels for 0%

commit v1 on v0

--- a/solution.py
+++ b/solution.py
@@ -13,7 +13,9 @@
     lat_rows = ensemble.shape[3]
     block_rows = lat_rows // lax.axis_size("member")
     row_offset = lax.axis_index("member") * block_rows
-    members = lax.all_to_all(ensemble, "member", split_axis=3, concat_axis=0, tiled=True)
+    parts = jnp.split(ensemble, lax.axis_size("member"), axis=3)
+    arrived = lax.all_to_all(jnp.stack(parts), "member", 0, 0)
+    members = jnp.concatenate(arrived, axis=0)
     all_flags = lax.all_gather(member_flags, "member", axis=0, tiled=True)
     slot_total = members.shape[0]
     truth_slice = lax.dynamic_slice_in_dim(observation, row_offset, block_rows, 2)

time: 101 us -> 112 us (1.11)
  local copies, waits for them, and re-layouts: 16.1 us -> 26.6 us
    unnamed x10 -> x16, local copies, waits for them, and re-layouts: 3.83 us -> 13.1 us
    another operation x0 -> x1, local copies, waits for them, and re-layouts: none -> 1.6 us  [on_device(): arrived = lax.all_to_all(jnp.stack(parts), 'member', 0, 0)]
  transfers between devices with their start and end apart: 1 -> 1, of which waited for: 0 -> 0; matrix products, arithmetic and copies ran while one was open for 2% -> 1% of each run, Pallas kernels for 0% -> 0%
where the time goes in v1:
time: 112 us; the launch traced here: 111 us
  blocking collectives  53.8 us (48%)
  local copies, waits for them, and re-layouts  26.6 us (24%)
  other arithmetic  21.6 us (19%)
  starting transfers between devices  5.2 us (5%)
  between operations  3.18 us (3%)
    psum x1, blocking collectives, on_device(): totals = lax.psum(partial_sums, ('member', 'lat'))  39.4 us
    unnamed x1, blocking collectives  14.4 us
    unnamed x16, local copies, waits for them, and re-layouts  13.1 us
    mul x16, other arithmetic, add_one(): one_flag * jnp.sum(flag_column * jnp.abs(one_slab - members), axis=0)  11.1 us
    dynamic_slice x16, local copies, waits for them, and re-layouts, add_one(): one_flag = lax.dynamic_index_in_dim(flags_here, position, 0, keepdims=False)  10.7 us
    reduce_sum x16, other arithmetic, add_one(): jnp.sum(flag_column * jnp.abs(one_slab - members), axis=0)  7.4 us
    all_to_all x1, starting transfers between devices, on_device(): arrived = lax.all_to_all(jnp.stack(parts), 'member', 0, 0)  5.2 us
  transfers between devices with their start and end apart: 1, of which 0 were waited for; matrix products, arithmetic and copies ran while one was open for 1% of the time, Pallas kernels for 0%

profile of v1, /device:TPU:0, one launch (start us, length us, event | category | flops | bytes accessed | tf_op | source)
XLA Modules:
  0.0 111.2 jit_solution(15184062010731343617)
XLA Ops:
  0.6 1.6 %bitcast_dynamic-update-slice_fusion.8 = f32[8,2,3,1,1,1440]{5,4,3,2,1,0:T(1,128)} fusion(f32[2,3,1,8,1440]{4,3,2,1,0:T(8,128)} %param.8), kind=kLoop, calls=%fused_computation.18 | loop fusion | bytes 71424
  2.3 1.6 %bitcast_dynamic-update-slice_fusion.7 = f32[8,2,3,1,1,1440]{5,4,3,2,1,0:T(1,128)} fusion(f32[8,2,3,1,1,1440]{5,4,3,2,1,0:T(1,128)} %bitcast_dynamic-update-slice_fusion.8, f32[2,3,1,8,1440]{4,3,2,1,0:T(8,128)} %param.8), kind=kLoop, calls=%fused_computation.17 | loop fusion | bytes 73728
  3.9 1.6 %bitcast_dynamic-update-slice_fusion.6 = f32[8,2,3,1,1,1440]{5,4,3,2,1,0:T(1,128)} fusion(f32[8,2,3,1,1,1440]{5,4,3,2,1,0:T(1,128)} %bitcast_dynamic-update-slice_fusion.7, f32[2,3,1,8,1440]{4,3,2,1,0:T(8,128)} %param.8), kind=kLoop, calls=%fused_computation.16 | loop fusion | bytes 73728
  5.5 1.6 %bitcast_dynamic-update-slice_fusion.5 = f32[8,2,3,1,1,1440]{5,4,3,2,1,0:T(1,128)} fusion(f32[8,2,3,1,1,1440]{5,4,3,2,1,0:T(1,128)} %bitcast_dynamic-update-slice_fusion.6, f32[2,3,1,8,1440]{4,3,2,1,0:T(8,128)} %param.8), kind=kLoop, calls=%fused_computation.15 | loop fusion | bytes 73728
  7.1 1.6 %bitcast_dynamic-update-slice_fusion.4 = f32[8,2,3,1,1,1440]{5,4,3,2,1,0:T(1,128)} fusion(f32[8,2,3,1,1,1440]{5,4,3,2,1,0:T(1,128)} %bitcast_dynamic-update-slice_fusion.5, f32[2,3,1,8,1440]{4,3,2,1,0:T(8,128)} %param.8), kind=kLoop, calls=%fused_computation.14 | loop fusion | bytes 73728
  8.7 1.6 %bitcast_dynamic-update-slice_fusion.3 = f32[8,2,3,1,1,1440]{5,4,3,2,1,0:T(1,128)} fusion(f32[8,2,3,1,1,1440]{5,4,3,2,1,0:T(1,128)} %bitcast_dynamic-update-slice_fusion.4, f32[2,3,1,8,1440]{4,3,2,1,0:T(8,128)} %param.8), kind=kLoop, calls=%fused_computation.13 | loop fusion | bytes 73728
  10.3 1.6 %bitcast_dynamic-update-slice_fusion.2 = f32[8,2,3,1,1,1440]{5,4,3,2,1,0:T(1,128)} fusion(f32[8,2,3,1,1,1440]{5,4,3,2,1,0:T(1,128)} %bitcast_dynamic-update-slice_fusion.3, f32[2,3,1,8,1440]{4,3,2,1,0:T(8,128)} %param.8), kind=kLoop, calls=%fused_computation.12 | loop fusion | bytes 73728
  11.9 1.6 %bitcast_dynamic-update-slice_fusion.1 = f32[8,2,3,1,1,1440]{5,4,3,2,1,0:T(1,128)} fusion(f32[8,2,3,1,1,1440]{5,4,3,2,1,0:T(1,128)} %bitcast_dynamic-update-slice_fusion.2, f32[2,3,1,8,1440]{4,3,2,1,0:T(8,128)} %param.8), kind=kLoop, calls=%fused_computation.11 | loop fusion | bytes 73728 | tf_op jit(solution)/shard_map/stack | solution.py:17
  13.5 5.2 %all-to-all-start = ((f32[8,2,3,1,1,1440]{5,4,3,2,1,0:T(1,128)}), f32[8,2,3,1,1,1440]{5,4,3,2,1,0:T(1,128)S(1)}, u32[]{:S(2)}, u32[]{:S(2)}) async-start(f32[8,2,3,1,1,1440]{5,4,3,2,1,0:T(1,128)} %bitcast_dynamic-update-slice_fusion.1), calls=%async_computation | async-start | bytes 589824 | tf_op jit(solution)/shard_map/all_to_all | solution.py:17
  18.7 0.6 copy-done.2
  19.3 0.6 dynamic-slice
  20.6 0.6 copy-done.1
  21.3 14.4 %all-reduce = f32[16]{0:T(128)S(1)} all-reduce(f32[16]{0:T(128)S(1)} %convert_dynamic-update-slice_fusion), channel_id=1, replica_groups=mesh['member'=8,'lat'=4] {'member'}, use_global_device_ids=true, to_apply=%add | all-reduce | flops 16 | bytes 128
  35.9 0.6 reduce_sum.50
  38.3 31.1 %while.25 = (s32[]{:T(128)}, f32[2,3,1,1,1440]{4,3,2,1,0:T(1,128)S(1)}, f32[2,8,3,1,1,1440]{5,4,3,2,1,0:T(1,128)S(1)}, f32[2,8]{1,0:T(2,128)S(1)}, f32[16,1,1,1,...) while((s32[]{:T(128)}, ...), condition=%wide.region_6.7_spmd, body=%wide.region_2.6_spmd.sunk | while | flops 285125 | bytes 780332 | solution.py:41
  38.4 15.4 %while.26 = (s32[]{:T(128)}, f32[3,1,1,1440]{3,2,1,0:T(1,128)S(1)}, f32[8]{0:T(128)S(1)}, f32[16,1,1,1,1]{0,4,3,2,1:T(1,128)S(1)}, f32[8,3,1,1,1440]{4,3,2,1,0:T...) while((s32[]{:T(128)}, f32[3,1,1,1440]{3,2,1,0:T(1,128)S(1)}, ...), condition=%wide.region_5.5_spmd.clone, body=%wide.region_3.4_spmd.clone.sunk | while | flops 285123 | bytes 466739 | solution.py:39
  38.5 0.5 multiply_reduce_fusion.4
  38.9 0.7 dynamic_slice.43
  39.6 0.7 broadcast_multiply_fusion.3
  40.4 0.5 multiply_reduce_fusion.4
  40.9 0.7 dynamic_slice.43
  41.5 0.7 broadcast_multiply_fusion.3
  42.8 0.7 dynamic_slice.43
  43.5 0.7 broadcast_multiply_fusion.3
  44.7 0.7 dynamic_slice.43
  45.4 0.7 broadcast_multiply_fusion.3
  46.2 0.5 multiply_reduce_fusion.4
  46.6 0.7 dynamic_slice.43
  47.3 0.7 broadcast_multiply_fusion.3
  48.1 0.5 multiply_reduce_fusion.4
  48.6 0.7 dynamic_slice.43
  49.2 0.7 broadcast_multiply_fusion.3
  50.5 0.7 dynamic_slice.43
  51.2 0.7 broadcast_multiply_fusion.3
  52.0 0.5 multiply_reduce_fusion.4
  52.4 0.7 dynamic_slice.43
  53.1 0.7 broadcast_multiply_fusion.3
  53.9 15.4 %while.26 = (s32[]{:T(128)}, f32[3,1,1,1440]{3,2,1,0:T(1,128)S(1)}, f32[8]{0:T(128)S(1)}, f32[16,1,1,1,1]{0,4,3,2,1:T(1,128)S(1)}, f32[8,3,1,1,1440]{4,3,2,1,0:T...) while((s32[]{:T(128)}, f32[3,1,1,1440]{3,2,1,0:T(1,128)S(1)}, ...), condition=%wide.region_5.5_spmd.clone, body=%wide.region_3.4_spmd.clone.sunk | while | flops 285123 | bytes 466739 | solution.py:39
  54.0 0.5 multiply_reduce_fusion.4
  54.5 0.7 dynamic_slice.43
  55.1 0.7 broadcast_multiply_fusion.3
  55.9 0.5 multiply_reduce_fusion.4
  56.4 0.7 dynamic_slice.43
  57.1 0.7 broadcast_multiply_fusion.3
  58.3 0.7 dynamic_slice.43
  59.0 0.7 broadcast_multiply_fusion.3
  59.8 0.5 multiply_reduce_fusion.4
  60.2 0.7 dynamic_slice.43
  60.9 0.7 broadcast_multiply_fusion.3
  61.7 0.5 multiply_reduce_fusion.4
  62.2 0.7 dynamic_slice.43
  62.8 0.7 broadcast_multiply_fusion.3
  64.1 0.7 dynamic_slice.43
  64.8 0.7 broadcast_multiply_fusion.3
  66.0 0.7 dynamic_slice.43
  66.7 0.7 broadcast_multiply_fusion.3
  67.5 0.5 multiply_reduce_fusion.4
  68.0 0.7 dynamic_slice.43
  68.6 0.7 broadcast_multiply_fusion.3
  69.5 0.5 multiply_reduce_fusion.1
  70.0 0.7 multiply_reduce_fusion.2
  70.6 0.6 sub.70
  71.3 39.4 %psum.7 = f32[3,1]{0,1:T(1,128)S(1)} all-reduce(f32[3,1]{0,1:T(1,128)S(1)} %bitcast.58), channel_id=1, replica_groups=mesh['member'=8,'lat'=4] {'member','lat'}, use_global_device_ids=true, to_apply=%region_9.10 | all-reduce | flops 3 | bytes 24 | tf_op jit(solution)/shard_map/psum | solution.py:48
  110.6 0.5 broadcast_multiply_fusion.1
  (75 shorter events, 4.3 us)
Async XLA Ops:
  0.6 35.8 %copy-start = (f32[3,1,8,1440]{3,2,1,0:T(8,128)S(1)}, f32[3,1,8,1440]{3,2,1,0:T(8,128)}, u32[]{:S(2)}) copy-start(f32[3,1,8,1440]{3,2,1,0:T(8,128)} %param.9) | copy-start | bytes 414724
  13.5 24.8 %all-to-all-start = ((f32[8,2,3,1,1,1440]{5,4,3,2,1,0:T(1,128)}), f32[8,2,3,1,1,1440]{5,4,3,2,1,0:T(1,128)S(1)}, u32[]{:S(2)}, u32[]{:S(2)}) async-start(f32[8,2,3,1,1,1440]{5,4,3,2,1,0:T(1,128)} %bitcast_dynamic-update-slice_fusion.1), calls=%async_computation | async-start | bytes 589824 | tf_op jit(solution)/shard_map/all_to_all | solution.py:17
  18.7 0.7 copy-start.2
  20.6 0.7 copy-start.1
